TPU v7x, 16 devices: a 4x2x1 block of a 4x4x8 slice. The times are simulated.
16 devices in a mesh: stage: 2 (over y, z), data: 8 (over x, core).
Axes of the slice: x: 4, y: 2, z: 1, core: 2. Of those that a mesh axis runs over, the one named last changes fastest.
The devices are a block of a 4x4x8 slice.
Arguments:
- w_master: float32 [16, 1024, 2048], P('stage', 'data'), parts along dimension 0
- momentum: float32 [16, 1024, 2048], P('stage', 'data'), parts along dimension 0
- grads: bfloat16 [16, 8, 1024, 2048], P(('stage', 'data')), parts along dimension 0
Outputs:
- output 1: float32 [16, 1024, 2048], P('stage', 'data'), parts along dimension 0
- output 2: float32 [16, 1024, 2048], P('stage', 'data'), parts along dimension 0
There are 2 independent parts. A program takes and returns all parts, laid end to end along the dimension named above; each array names one.
All inputs are finite; a program needn't handle non-finite values.
Results may differ from a plain program's by a relative error of at most 0.0103596.
Values are sent between devices in bfloat16 or wider.
A program may use at most 768 MiB of HBM per device.

v0:
```python
import math
import jax
import jax.numpy as jnp
from jax import lax
from jax.sharding import PartitionSpec as P, NamedSharding

MOMENTUM_COEF = 0.95
LEARN_RATE = 0.05
WEIGHT_DECAY = 0.2
NORM_EPS = 1e-7
COEF_A = 3.4445
COEF_B = -4.7750
COEF_C = 2.0315
NS_ITERS = 5


def newton_schulz(x_cur):
    n_rows, n_cols = x_cur.shape[1], x_cur.shape[2]
    for _ in range(NS_ITERS):
        if n_rows > n_cols:
            gram_f = jnp.einsum('bri,brj->bij', x_cur, x_cur, preferred_element_type=jnp.float32)
        else:
            gram_f = jnp.einsum('bik,bjk->bij', x_cur, x_cur, preferred_element_type=jnp.float32)
        gram_mat = gram_f.astype(jnp.bfloat16)
        gram_sq = jnp.einsum('bij,bjk->bik', gram_mat, gram_mat, preferred_element_type=jnp.float32)
        poly_mat = (COEF_B * gram_mat.astype(jnp.float32) + COEF_C * gram_sq).astype(jnp.bfloat16)
        if n_rows > n_cols:
            poly_x = jnp.einsum('brj,bij->bri', x_cur, poly_mat, preferred_element_type=jnp.float32)
        else:
            poly_x = jnp.einsum('bij,bjk->bik', poly_mat, x_cur, preferred_element_type=jnp.float32)
        x_cur = (COEF_A * x_cur.astype(jnp.float32) + poly_x).astype(jnp.bfloat16)
    return x_cur


def solution(mesh):
    group_size = mesh.shape['data']
    row_spec = P('stage', 'data', None)
    grad_spec = P(('stage', 'data'), None, None, None)

    def local_step(w_rows, mom_rows, grad_full):
        n_mats, rows_dev, n_cols = w_rows.shape
        n_rows = rows_dev * group_size
        per_dev = n_mats // group_size
        my_index = lax.axis_index('data')
        grad_rows = lax.psum_scatter(grad_full[0].astype(jnp.float32), 'data', scatter_dimension=1, tiled=True)
        mom_new = MOMENTUM_COEF * mom_rows + grad_rows
        frob_norm = jnp.sqrt(lax.psum(jnp.sum(mom_new * mom_new, axis=(1, 2)), 'data'))
        owned_mom = lax.all_to_all(mom_new.astype(jnp.bfloat16), 'data', 0, 1, tiled=True)
        owned_norm = lax.dynamic_slice_in_dim(frob_norm, my_index * per_dev, per_dev)
        x_start = (owned_mom.astype(jnp.float32) / (owned_norm[:, None, None] + NORM_EPS)).astype(jnp.bfloat16)
        x_ortho = newton_schulz(x_start)
        x_rows = lax.all_to_all(x_ortho, 'data', 1, 0, tiled=True)
        rms_scale = 0.2 * math.sqrt(max(n_rows, n_cols))
        w_new = w_rows - LEARN_RATE * (x_rows.astype(jnp.float32) * rms_scale + WEIGHT_DECAY * w_rows)
        return w_new, mom_new

    return jax.shard_map(local_step, mesh=mesh, in_specs=(row_spec, row_spec, grad_spec), out_specs=(row_spec, row_spec), check_vma=False)
```

profile of v0, /device:TPU:113, one launch (start us, length us, event | category | flops | bytes accessed | tf_op | source)
XLA Modules:
  0.0 689.8 jit_solution(16408991248800751370)
XLA Ops:
  7.2 0.1 reduce-scatter.2.cloned.1.call-start
  7.2 32.4 %bitcast_convert_fusion = f32[8,1024,2048]{2,1,0:T(8,128)} fusion(bf16[1,8,1024,2048]{3,2,1,0:T(8,128)(2,1)} %param.5), kind=kLoop, calls=%fused_computation | loop fusion | flops 16777216 | bytes 100663296 | tf_op jit(solution)/shard_map/convert_element_type | solution.py:45
  39.7 0.1 reduce-scatter.2.cloned.1.call-update
  39.7 326.4 %reduce-scatter.2.cloned.1.call-done = f32[8,128,2048]{2,1,0:T(8,128)} async-done(((f32[8,1024,2048]{2,1,0:T(8,128)}), f32[8,128,2048]{2,1,0:T(8,128)}) %reduce-scatter.2.cloned.1.call-update) | async-done | bytes 8388624 | tf_op jit(solution)/shard_map/reduce_scatter | solution.py:45
  366.1 10.8 %multiply_reduce_fusion = (f32[8]{0:T(128)S(1)}, f32[8,128,2048]{2,1,0:T(8,128)}) fusion(f32[8,128,2048]{2,1,0:T(8,128)} %reduce-scatter.2.cloned.1.call-done, f32[8,128,2048]{2,1,0:T(8,128)} %param.4), kind=kLoop, calls=%fused_computation.9 | loop fusion | flops 8388600 | bytes 25165856 | tf_op jit(solution)/shard_map/reduce_sum | solution.py:47
  376.9 6.0 convert_element_type.146
  383.0 5.5 all-to-all-start
  388.5 53.1 %psum.7 = f32[8]{0:T(128)S(1)} all-reduce(f32[8]{0:T(128)S(1)} %get-tuple-element.2), channel_id=1, replica_groups=mesh['stage'=2,'data'=8] {'data'}, use_global_device_ids=true, to_apply=%region_2.0 | all-reduce | flops 8 | bytes 64 | tf_op jit(solution)/shard_map/psum | solution.py:47
  441.6 0.6 dynamic_slice.3
  442.9 0.0 all-to-all-done
  442.9 3.2 divide_convert_fusion
  446.1 0.0 copy-start
  446.1 2.0 copy-done
  448.1 4.7 fusion.26
  452.8 11.5 %add_convert_fusion.4 = bf16[1024,2048]{1,0:T(8,128)(2,1)} fusion(bf16[1024,2048]{1,0:T(8,128)(2,1)} %bitcast.41, bf16[1024,1024]{1,0:T(8,128)(2,1)S(1)} %fusion.26), kind=kOutput, calls=%fused_computation.7 | convolution fusion | flops 6456082432 | bytes 10485760 | tf_op jit(solution)/shard_map/bij,bjk->bik/dot_general | solution.py:30
  464.4 8.0 %fusion.27 = bf16[1024,1024]{1,0:T(8,128)(2,1)S(1)} fusion(bf16[1024,2048]{1,0:T(8,128)(2,1)} %add_convert_fusion.4), kind=kOutput, calls=%fused_computation.34 | convolution fusion | flops 4294967296 | bytes 6291456 | tf_op jit(solution)/shard_map/bik,bjk->bij/dot_general | solution.py:23
  472.4 11.8 %add_convert_fusion.3 = bf16[1024,2048]{1,0:T(8,128)(2,1)} fusion(bf16[1024,2048]{1,0:T(8,128)(2,1)} %add_convert_fusion.4, bf16[1024,1024]{1,0:T(8,128)(2,1)S(1)} %fusion.27), kind=kOutput, calls=%fused_computation.6 | convolution fusion | flops 6456082432 | bytes 10485760 | tf_op jit(solution)/shard_map/bij,bjk->bik/dot_general | solution.py:30
  484.1 8.0 %fusion.28 = bf16[1024,1024]{1,0:T(8,128)(2,1)S(1)} fusion(bf16[1024,2048]{1,0:T(8,128)(2,1)} %add_convert_fusion.3), kind=kOutput, calls=%fused_computation.35 | convolution fusion | flops 4294967296 | bytes 6291456 | tf_op jit(solution)/shard_map/bik,bjk->bij/dot_general | solution.py:23
  492.1 11.6 %add_convert_fusion.2 = bf16[1024,2048]{1,0:T(8,128)(2,1)} fusion(bf16[1024,2048]{1,0:T(8,128)(2,1)} %add_convert_fusion.3, bf16[1024,1024]{1,0:T(8,128)(2,1)S(1)} %fusion.28), kind=kOutput, calls=%fused_computation.5 | convolution fusion | flops 6456082432 | bytes 10485760 | tf_op jit(solution)/shard_map/bij,bjk->bik/dot_general | solution.py:30
  503.7 8.0 %fusion.29 = bf16[1024,1024]{1,0:T(8,128)(2,1)S(1)} fusion(bf16[1024,2048]{1,0:T(8,128)(2,1)} %add_convert_fusion.2), kind=kOutput, calls=%fused_computation.36 | convolution fusion | flops 4294967296 | bytes 6291456 | tf_op jit(solution)/shard_map/bik,bjk->bij/dot_general | solution.py:23
  511.7 11.8 %add_convert_fusion.1 = bf16[1024,2048]{1,0:T(8,128)(2,1)} fusion(bf16[1024,2048]{1,0:T(8,128)(2,1)} %add_convert_fusion.2, bf16[1024,1024]{1,0:T(8,128)(2,1)S(1)} %fusion.29), kind=kOutput, calls=%fused_computation.4 | convolution fusion | flops 6456082432 | bytes 10485760 | tf_op jit(solution)/shard_map/bij,bjk->bik/dot_general | solution.py:30
  523.5 8.0 %fusion.30 = bf16[1024,1024]{1,0:T(8,128)(2,1)S(1)} fusion(bf16[1024,2048]{1,0:T(8,128)(2,1)} %add_convert_fusion.1), kind=kOutput, calls=%fused_computation.37 | convolution fusion | flops 4294967296 | bytes 6291456 | tf_op jit(solution)/shard_map/bik,bjk->bij/dot_general | solution.py:23
  531.5 11.5 %fusion = bf16[1,1024,2048]{2,1,0:T(8,128)(2,1)} fusion(bf16[1024,2048]{1,0:T(8,128)(2,1)} %add_convert_fusion.1, bf16[1024,1024]{1,0:T(8,128)(2,1)S(1)} %fusion.30), kind=kOutput, calls=%fused_computation.11 | convolution fusion | flops 6456082432 | bytes 10485760 | tf_op jit(solution)/shard_map/bij,bjk->bik/dot_general | solution.py:30
  543.0 8.6 %copy.8 = bf16[1,1024,2048]{2,0,1:T(2,128)(2,1)} copy(bf16[1,1024,2048]{2,1,0:T(8,128)(2,1)} %fusion) | data formatting | bytes 8388608 | tf_op jit(solution)/shard_map/convert_element_type | solution.py:31
  551.6 0.5 broadcast.76
  552.1 26.6 %reduce = bf16[1024,2048]{1,0:T(8,128)(2,1)} reduce(bf16[1024,1,2048]{2,1,0:T(2,128)(2,1)} %bitcast.39, bf16[]{:T(256)} %broadcast.76), dimensions={1}, to_apply=%bitcast.37.reduce_sub_computation | reduce | bytes 8388610
  578.8 7.8 %reshape.164 = bf16[8,2,131072]{2,1,0:T(2,128)(2,1)} reshape(bf16[1024,2048]{1,0:T(8,128)(2,1)} %reduce) | data formatting | bytes 8388608
  586.6 54.8 %all_to_all.8 = bf16[8,2,131072]{2,1,0:T(2,128)(2,1)} all-to-all(bf16[8,2,131072]{2,1,0:T(2,128)(2,1)} %reshape.164), channel_id=1, replica_groups=mesh['stage'=2,'data'=8] {'data'}, dimensions={0} | all-to-all | bytes 8388608 | tf_op jit(solution)/shard_map/all_to_all | solution.py:52
  641.3 8.7 %reshape.165 = bf16[1024,1,2048]{2,1,0:T(2,128)(2,1)} reshape(bf16[8,2,131072]{2,1,0:T(2,128)(2,1)} %all_to_all.8) | data formatting | bytes 8388608
  650.1 12.9 %convert_multiply_fusion = f32[1,1024,2048]{2,0,1:T(1,128)S(1)} fusion(bf16[1024,1,2048]{2,1,0:T(2,128)(2,1)} %reshape.165), kind=kLoop, calls=%fused_computation.2 | loop fusion | flops 4194304 | bytes 12582912 | tf_op jit(solution)/shard_map/mul | solution.py:54
  662.9 7.5 %copy.6 = f32[1,1024,2048]{2,1,0:T(8,128)} copy(f32[1,1024,2048]{2,0,1:T(1,128)S(1)} %convert_multiply_fusion) | data formatting | bytes 16777216
  670.4 12.2 %multiply_subtract_fusion = f32[8,128,2048]{2,1,0:T(8,128)} fusion(f32[8,128,2048]{2,1,0:T(8,128)} %param.3, f32[8,128,2048]{2,1,0:T(8,128)} %bitcast.38), kind=kLoop, calls=%fused_computation.1 | loop fusion | flops 8388608 | bytes 25165824 | tf_op jit(solution)/shard_map/sub | solution.py:54
  (1 shorter events, 0.0 us)
Async XLA Ops:
  7.2 358.9 %reduce-scatter.2.cloned.1.call-start = ((), (), s32[]{:S(2)}) async-start(), calls=%async_computation.3 | async-start | bytes 75497472 | tf_op jit(solution)/shard_map/reduce_scatter | solution.py:45
  383.0 59.9 %all-to-all-start = ((bf16[8,128,2048]{2,1,0:T(8,128)(2,1)}), bf16[8,128,2048]{2,1,0:T(8,128)(2,1)}, u32[]{:S(2)}, u32[]{:S(2)}) async-start(bf16[8,128,2048]{2,1,0:T(8,128)(2,1)} %convert_element_type.146), calls=%async_computation.1 | async-start | bytes 8388608 | tf_op jit(solution)/shard_map/all_to_all | solution.py:48
  446.1 2.0 copy-start
Sparse Core Ops, SparseCore 0:
  39.9 326.1 reduce-scatter.1
where the time goes:
time: 694 us; the launch traced here: 690 us
  waiting for transfers between devices  326 us (47%)
  blocking collectives  108 us (16%)
  other arithmetic  104 us (15%)
  matrix products  94.9 us (14%)
  local copies, waits for them, and re-layouts  35.8 us (5%)
  between operations  15 us (2%)
    reduce_scatter x1, waiting for transfers between devices, local_step(): lax.psum_scatter(grad_full[0].astype(jnp.float32), 'data', scatter_dimens...  326 us
    dot_general x5, matrix products, newton_schulz(): jnp.einsum('bij,bjk->bik', poly_mat, x_cur, preferred_element_type=jnp.fl...  58.2 us
    all_to_all x1, blocking collectives, local_step(): x_rows = lax.all_to_all(x_ortho, 'data', 1, 0, tiled=True)  54.8 us
    psum x1, blocking collectives, local_step(): lax.psum(jnp.sum(mom_new * mom_new, axis=(1, 2)), 'data')  53.1 us
    dot_general x5, matrix products, newton_schulz(): jnp.einsum('bik,bjk->bij', x_cur, x_cur, preferred_element_type=jnp.float32)  36.7 us
    convert_element_type x1, other arithmetic, local_step(): grad_full[0].astype(jnp.float32)  32.4 us
    unnamed x1, other arithmetic  26.6 us
    unnamed x6, local copies, waits for them, and re-layouts  26.6 us
  transfers between devices with their start and end apart: 2, of which 1 were waited for; matrix products, arithmetic and copies ran while one was open for 0% of the time, Pallas kernels for 0%

commit v1 on v0

v1 whole, which is shorter than its diff:
```python
import functools
import math
import jax
import jax.numpy as jnp
from jax import lax
from jax.experimental import pallas as pl
from jax.experimental.pallas import tpu as pltpu
from jax.sharding import PartitionSpec as P

MOMENTUM_COEF = 0.95
LEARN_RATE = 0.05
WEIGHT_DECAY = 0.2
NORM_EPS = 1e-7
COEF_A = 3.4445
COEF_B = -4.7750
COEF_C = 2.0315
NS_ITERS = 5

CORES = 2
AHEAD = 3
CHUNK = 32
ITERS_PER_STEP = 2
MESH = pl.DeviceIdType.MESH
F32 = jnp.float32
BF16 = jnp.bfloat16


def fused_kernel(group, scale, w_ref, mom_ref, g_ref, w_out, mom_out,
                 mg, fin, fsum, own, mout, momin, xmat, gram, poly, ret, nsend, ninbox,
                 s_mg, s_fin, s_fsum, s_own, s_mout, s_mom, s_x, s_n, s_ret,
                 s_gsend, s_xsend, s_nsend, s_rsend, s_momout, s_wload, s_wout):
    n_mats, rows, cols = w_ref.shape
    half = rows // 2
    chips = group // CORES
    n_rows = rows * group
    me = lax.axis_index("data")
    chip, core = me // CORES, me % CORES
    right, left, far = (chip + 1) % chips, (chip + chips - 1) % chips, (chip + 2) % chips

    def dev(a_chip, a_core):
        return a_chip * CORES + a_core

    def owner_of(m):
        return dev(m % chips, m // chips)

    my_mat = (me % CORES) * chips + chip

    def grad_rows(m, a_chip, a_core, h):
        start = pl.multiple_of(dev(a_chip, a_core) * rows + h * half, half)
        return g_ref.at[0, m, pl.ds(start, half)]

    def remote(src, dst, send, recv, to):
        return pltpu.make_async_remote_copy(src_ref=src, dst_ref=dst, send_sem=send, recv_sem=recv,
                                            device_id={"data": to}, device_id_type=MESH)

    def wait_bytes(ref, sem):
        pltpu.make_async_copy(ref, ref, sem).wait()

    def issue_raw(m):
        send = s_gsend.at[m]
        for kk in range(CORES):
            remote(grad_rows(m, far, kk, 0), mg.at[m, 0, core], send, s_mg.at[m, 0], dev(right, kk)).start()
            remote(grad_rows(m, far, kk, 1), mg.at[m, 1, core], send, s_mg.at[m, 1], dev(left, kk)).start()
        mate = dev(chip, 1 - core)
        remote(grad_rows(m, right, 1 - core, 0), mg.at[m, 0, 2], send, s_mg.at[m, 0], mate).start()
        remote(grad_rows(m, left, 1 - core, 1), mg.at[m, 1, 2], send, s_mg.at[m, 1], mate).start()
        for kk in range(CORES):
            remote(grad_rows(m, right, kk, 1), fin.at[m, 1, core], send, s_fin.at[m], dev(right, kk)).start()
            remote(grad_rows(m, left, kk, 0), fin.at[m, 0, core], send, s_fin.at[m], dev(left, kk)).start()
        for h in range(2):
            remote(grad_rows(m, chip, 1 - core, h), fin.at[m, h, 2], send, s_fin.at[m], mate).start()

    def load_own(m):
        slot = m % 3
        pltpu.make_async_copy(grad_rows(m, right, core, 0), own.at[slot, 0], s_own.at[slot]).start()
        pltpu.make_async_copy(grad_rows(m, left, core, 1), own.at[slot, 1], s_own.at[slot]).start()
        for h in range(2):
            pltpu.make_async_copy(grad_rows(m, chip, core, h), own.at[slot, 2 + h], s_own.at[slot]).start()

    def merge_copy(m, h):
        to = dev(right if h == 0 else left, core)
        return remote(mout.at[m % 2, h], fsum.at[m, h], s_mout.at[m % 2, h], s_fsum.at[m, h], to)

    def merge(m):
        slot = m % 3
        wait_bytes(own.at[slot], s_own.at[slot])
        for h in range(2):
            wait_bytes(mg.at[m, h], s_mg.at[m, h])

            @pl.when(m >= 2)
            def _():
                merge_copy(m - 2, h).wait_send()

            @pl.loop(0, half // min(CHUNK, half))
            def _(i):
                size = min(CHUNK, half)
                at = pl.ds(pl.multiple_of(i * size, size), size)
                total = own[slot, h, at].astype(F32) + mg[m, h, 2, at].astype(F32)
                total = total + (mg[m, h, 0, at].astype(F32) + mg[m, h, 1, at].astype(F32))
                mout[m % 2, h, at] = total
            merge_copy(m, h).start()

    def forward_copies(m):
        to = owner_of(m)
        out = []
        for h in range(2):
            at = pl.ds(pl.multiple_of(me * rows + h * half, half), half)
            out.append((fin.at[m, h, 0], xmat.at[at]))
        return to, out

    def finish(m):
        slot = m % 3
        wait_bytes(fin.at[m], s_fin.at[m])
        wait_bytes(momin.at[m % 2], s_mom.at[m % 2])
        size = min(CHUNK, half)
        acc = jnp.zeros((8, 128), F32)
        for h in range(2):
            wait_bytes(fsum.at[m, h], s_fsum.at[m, h])

            def part(i, acc):
                at = pl.ds(pl.multiple_of(i * size, size), size)
                mom_at = pl.ds(pl.multiple_of(h * half + i * size, size), size)
                total = own[slot, 2 + h, at].astype(F32) + fin[m, h, 2, at].astype(F32)
                total = total + (fin[m, h, 0, at].astype(F32) + fin[m, h, 1, at].astype(F32))
                total = total + fsum[m, h, at]
                new = MOMENTUM_COEF * momin[m % 2, mom_at] + total
                fsum[m, h, at] = new
                fin[m, h, 0, at] = new.astype(BF16)
                square = new * new
                for r in range(0, size, 8):
                    for q in range(0, cols, 128):
                        acc = acc + square[r:r + 8, q:q + 128]
                return acc

            acc = lax.fori_loop(0, half // size, part, acc)
            pltpu.make_async_copy(fsum.at[m, h], mom_out.at[m, pl.ds(h * half, half)], s_momout.at[m]).start()
        nsend[m] = acc
        to, copies = forward_copies(m)

        @pl.when(to == me)
        def _():
            for src, dst in copies:
                pltpu.make_async_copy(src, dst, s_x).start()
            pltpu.make_async_copy(nsend.at[m], ninbox.at[me], s_n).start()

        @pl.when(to != me)
        def _():
            for src, dst in copies:
                remote(src, dst, s_xsend.at[m], s_x, to).start()
            remote(nsend.at[m], ninbox.at[me], s_nsend.at[m], s_n, to).start()

    def w_load(m):
        wait_bytes(fsum.at[m], s_momout.at[m])
        for h in range(2):
            pltpu.make_async_copy(w_ref.at[m, pl.ds(h * half, half)], fsum.at[m, h], s_wload.at[m]).start()

    def ns_begin():
        wait_bytes(xmat, s_x)
        wait_bytes(ninbox, s_n)
        total = jnp.sum(ninbox[...], axis=0)
        total = jnp.sum(jnp.sum(total, axis=0, keepdims=True), axis=1, keepdims=True)
        bound = jnp.sqrt(total) + NORM_EPS

        @pl.loop(0, n_rows // CHUNK)
        def _(i):
            at = pl.ds(pl.multiple_of(i * CHUNK, CHUNK), CHUNK)
            xmat[at] = (xmat[at].astype(F32) / bound).astype(BF16)

    def ns_iter():
        wide = min(512, n_rows)

        @pl.loop(0, n_rows // wide)
        def _(j):
            at = pl.ds(pl.multiple_of(j * wide, wide), wide)
            prod = lax.dot_general(xmat[...], xmat[at, :], (((1,), (1,)), ((), ())), preferred_element_type=F32)
            gram[:, at] = prod.astype(BF16)

        @pl.loop(0, n_rows // wide)
        def _(j):
            at = pl.ds(pl.multiple_of(j * wide, wide), wide)
            prod = jnp.dot(gram[...], gram[:, at], preferred_element_type=F32)
            poly[:, at] = (COEF_B * gram[:, at].astype(F32) + COEF_C * prod).astype(BF16)

        wide_x = min(512, cols)

        @pl.loop(0, cols // wide_x)
        def _(j):
            at = pl.ds(pl.multiple_of(j * wide_x, wide_x), wide_x)
            prod = jnp.dot(poly[...], xmat[:, at], preferred_element_type=F32)
            xmat[:, at] = (COEF_A * xmat[:, at].astype(F32) + prod).astype(BF16)

    def iters_done(s):
        early = jnp.clip(ITERS_PER_STEP * (s - my_mat - 2), 0, NS_ITERS)
        return jnp.where(s >= n_mats, NS_ITERS, early)

    barrier = pltpu.get_barrier_semaphore()
    for i in range(1, group):
        pl.semaphore_signal(barrier, inc=1, device_id={"data": (me + i) % group}, device_id_type=MESH)
    pl.semaphore_wait(barrier, group - 1)

    @pl.loop(0, AHEAD)
    def _(m):
        issue_raw(m)
    load_own(0)

    @pl.loop(0, n_mats + 1)
    def _(s):
        @pl.when(s + AHEAD < n_mats)
        def _():
            issue_raw(s + AHEAD)

        @pl.when(s + 1 < n_mats)
        def _():
            load_own(s + 1)

        @pl.when(s < n_mats)
        def _():
            pltpu.make_async_copy(mom_ref.at[s], momin.at[s % 2], s_mom.at[s % 2]).start()
            merge(s)

        @pl.when(s >= 1)
        def _():
            finish(s - 1)

        @pl.when(s >= 2)
        def _():
            w_load(s - 2)

        lo, hi = iters_done(s - 1), iters_done(s)

        @pl.when((lo == 0) & (hi > 0))
        def _():
            ns_begin()

        def run(i, carry):
            ns_iter()
            return carry
        lax.fori_loop(lo, hi, run, 0)

    w_load(n_mats - 1)

    pltpu.make_async_copy(xmat.at[pl.ds(pl.multiple_of(me * rows, rows), rows)], ret.at[my_mat], s_ret.at[my_mat]).start()
    for i in range(1, group):
        to = (me + i) % group
        remote(xmat.at[pl.ds(pl.multiple_of(to * rows, rows), rows)], ret.at[my_mat], s_rsend, s_ret.at[my_mat], to).start()

    @pl.loop(0, n_mats)
    def _(m):
        wait_bytes(ret.at[m], s_ret.at[m])
        wait_bytes(fsum.at[m], s_wload.at[m])
        size = min(CHUNK, half)
        for h in range(2):
            @pl.loop(0, half // size)
            def _(i):
                at = pl.ds(pl.multiple_of(i * size, size), size)
                ret_at = pl.ds(pl.multiple_of(h * half + i * size, size), size)
                w = fsum[m, h, at]
                fsum[m, h, at] = w - LEARN_RATE * (ret[m, ret_at].astype(F32) * scale + WEIGHT_DECAY * w)
            pltpu.make_async_copy(fsum.at[m, h], w_out.at[m, pl.ds(h * half, half)], s_wout.at[m]).start()

    @pl.loop(0, n_mats)
    def _(m):
        done = g_ref.at[0, m, pl.ds(0, 12 * half)]
        wait_bytes(done, s_gsend.at[m])
        wait_bytes(fsum.at[m], s_wout.at[m])

        @pl.when(owner_of(m) != me)
        def _():
            wait_bytes(ret.at[m], s_xsend.at[m])
            wait_bytes(nsend.at[m], s_nsend.at[m])
    for m in range(n_mats - 2, n_mats):
        for h in range(2):
            merge_copy(m, h).wait_send()
    wait_bytes(xmat.at[pl.ds(0, (group - 1) * rows)], s_rsend)


def solution(mesh):
    group = mesh.shape['data']
    row_spec = P('stage', 'data', None)
    grad_spec = P(('stage', 'data'), None, None, None)

    def local_step(w_rows, mom_rows, grad_full):
        n_mats, rows, cols = w_rows.shape
        half = rows // 2
        n_rows = rows * group
        scale = 0.2 * math.sqrt(max(n_rows, cols))
        hbm = pl.BlockSpec(memory_space=pl.ANY)
        dma = pltpu.SemaphoreType.DMA
        flops = NS_ITERS * (4 * n_rows * n_rows * cols + 2 * n_rows ** 3)
        return pl.pallas_call(
            functools.partial(fused_kernel, group, scale),
            out_shape=(jax.ShapeDtypeStruct(w_rows.shape, F32), jax.ShapeDtypeStruct(w_rows.shape, F32)),
            in_specs=[hbm] * 3,
            out_specs=(hbm, hbm),
            scratch_shapes=[
                pltpu.VMEM((n_mats, 2, 3, half, cols), BF16),
                pltpu.VMEM((n_mats, 2, 3, half, cols), BF16),
                pltpu.VMEM((n_mats, 2, half, cols), F32),
                pltpu.VMEM((3, 4, half, cols), BF16),
                pltpu.VMEM((2, 2, half, cols), F32),
                pltpu.VMEM((2, rows, cols), F32),
                pltpu.VMEM((n_rows, cols), BF16),
                pltpu.VMEM((n_rows, n_rows), BF16),
                pltpu.VMEM((n_rows, n_rows), BF16),
                pltpu.VMEM((n_mats, rows, cols), BF16),
                pltpu.VMEM((n_mats, 8, 128), F32),
                pltpu.VMEM((group, 8, 128), F32),
                dma((n_mats, 2)), dma((n_mats,)), dma((n_mats, 2)), dma((3,)), dma((2, 2)), dma((2,)),
                dma, dma, dma((n_mats,)),
                dma((n_mats,)), dma((n_mats,)), dma((n_mats,)), dma, dma((n_mats,)), dma((n_mats,)), dma((n_mats,)),
            ],
            compiler_params=pltpu.CompilerParams(collective_id=0, has_side_effects=True, vmem_limit_bytes=67043328),
            cost_estimate=pl.CostEstimate(flops=flops, bytes_accessed=2 ** 26, transcendentals=0),
            name="muon_step",
        )(w_rows, mom_rows, grad_full)

    return jax.shard_map(local_step, mesh=mesh, in_specs=(row_spec, row_spec, grad_spec), out_specs=(row_spec, row_spec), check_vma=False)
```

time: 694 us -> 457 us (0.66)
  Pallas kernels: 0 us -> 436 us
  waiting for transfers between devices: 326 us -> 0 us
  blocking collectives: 108 us -> 0 us
  other arithmetic: 104 us -> 0 us
  matrix products: 94.9 us -> 0 us
  local copies, waits for them, and re-layouts: 35.8 us -> 11.4 us
  between operations: 15 us -> 0.65 us
    pallas_call x0 -> x1, Pallas kernels: none -> 436 us  [local_step(): pl.pallas_call(functools.partial(fused_kernel, group, scale), out_shape=(...]
    reduce_scatter x1 -> x0, waiting for transfers between devices: 326 us -> none  [local_step(): lax.psum_scatter(grad_full[0].astype(jnp.float32), 'data', scatter_dimens...]
    dot_general x10 -> x0, matrix products: 94.9 us -> none  [the longest x5 58.2 us: newton_schulz(): jnp.einsum('bij,bjk->bik', poly_mat, x_cur, preferred_element_type=jnp.fl...]
    all_to_all x1 -> x0, blocking collectives: 54.8 us -> none  [local_step(): x_rows = lax.all_to_all(x_ortho, 'data', 1, 0, tiled=True)]
    psum x1 -> x0, blocking collectives: 53.1 us -> none  [local_step(): lax.psum(jnp.sum(mom_new * mom_new, axis=(1, 2)), 'data')]
    convert_element_type x3 -> x0, other arithmetic: 41.7 us -> none  [the longest x1 32.4 us: local_step(): grad_full[0].astype(jnp.float32)]
    unnamed x1 -> x0, other arithmetic: 26.6 us -> none
    unnamed x6 -> x4, local copies, waits for them, and re-layouts: 26.6 us -> 11.4 us
  transfers between devices with their start and end apart: 2 -> 0, of which waited for: 1 -> 0; matrix products, arithmetic and copies ran while one was open for 0% -> 0% of each run, Pallas kernels for 0% -> 0%
where the time goes in v1:
time: 457 us; the launch traced here: 448 us
  Pallas kernels  436 us (95%)
  local copies, waits for them, and re-layouts  11.4 us (2%)
    pallas_call x1, Pallas kernels, local_step(): pl.pallas_call(functools.partial(fused_kernel, group, scale), out_shape=(...  436 us
    unnamed x4, local copies, waits for them, and re-layouts  11.4 us

profile of v1, /device:TPU:113, one launch (start us, length us, event | category | flops | bytes accessed | tf_op | source)
XLA Modules:
  0.0 448.5 jit_solution(15077200832026413248)
XLA Ops:
  0.6 436.4 %muon_step.1 = (f32[8,128,2048]{2,1,0:T(8,128)}, f32[8,128,2048]{2,1,0:T(8,128)}) custom-call(f32[8,128,2048]{2,1,0:T(8,128)} %w_ref.1, f32[8,128,2048]{2,1,0:T(8,128)} %mom_ref.1, bf16[1,8,1024,2048]{3,2,1,0:T(8,128)(2,1)} %g_ref.1), custom_call_target="tpu_custom_call" | custom-call | flops 53687091200 | bytes 67108864 | tf_op jit(solution)/shard_map/muon_step/pallas_call | solution.py:290
  437.0 0.0 copy-start
  437.0 8.0 %copy.7 = f32[8,128,2048]{2,1,0:T(8,128)} copy(f32[8,128,2048]{2,1,0:T(8,128)} %get-tuple-element.4) | data formatting | bytes 16777216
  445.1 0.0 copy-done
  445.1 3.4 copy.8
Async XLA Ops:
  437.0 8.1 %copy-start = (f32[8,128,2048]{2,1,0:T(8,128)S(1)}, f32[8,128,2048]{2,1,0:T(8,128)}, u32[]{:S(2)}) copy-start(f32[8,128,2048]{2,1,0:T(8,128)} %get-tuple-element.5) | copy-start | bytes 25165828
